TPU v7x, 32 devices: a whole 2x2x4 slice. The times are simulated.
32 devices in a mesh: zero: 8 (over z, y), tp: 4 (over x, core).
Axes of the slice: x: 2, y: 2, z: 4, core: 2. Of those that a mesh axis runs over, the one named last changes fastest.
Arguments:
- train_gate: bfloat16 [3072, 8192], P('zero', 'tp'), may hold values from -0.109375 to 0.109375
- low_gate: bfloat16 [3072, 16], P('zero'), may hold values from -0.109375 to 0.109375
- high_gate: bfloat16 [16, 8192], P(None, 'tp'), may hold values from -1.5 to 1.5
- train_up: bfloat16 [3072, 8192], P('zero', 'tp'), may hold values from -0.109375 to 0.109375
- low_up: bfloat16 [3072, 16], P('zero'), may hold values from -0.109375 to 0.109375
- high_up: bfloat16 [16, 8192], P(None, 'tp'), may hold values from -1.5 to 1.5
- train_down: bfloat16 [8192, 3072], P('tp', 'zero'), may hold values from -0.0625 to 0.0625
- low_down: bfloat16 [8192, 16], P('tp'), may hold values from -0.0625 to 0.0625
- high_down: bfloat16 [16, 3072], P(None, 'zero'), may hold values from -1.5 to 1.5
- norm_train: float32 [3072], P(('zero', 'tp')), may hold values from 0.25 to 1.75
- norm_step: float32 [3072], P(('zero', 'tp')), may hold values from -0.3 to 0.3
Outputs:
- serve_gate: bfloat16 [8192, 3072], P('tp')
- serve_up: bfloat16 [8192, 3072], P('tp')
- serve_down: bfloat16 [3072, 8192], P(None, 'tp')
- serve_norm: bfloat16 [3072], replicated
All inputs are finite; a program needn't handle non-finite values.
Results may differ from a plain program's by a relative error of at most 0.001.
Values may be sent and summed in bfloat16 or wider, within the bound.
A program may use at most 128 MiB of HBM per device.

v0:
```python
import jax
import jax.numpy as jnp
from jax import lax
from jax.sharding import PartitionSpec as P

mix_rate = 0.5


def per_device(
    train_gate,
    low_gate,
    high_gate,
    train_up,
    low_up,
    high_up,
    train_down,
    low_down,
    high_down,
    norm_train,
    norm_step,
):
    fresh_gate = train_gate.astype(jnp.float32) + mix_rate * jnp.dot(
        low_gate, high_gate, preferred_element_type=jnp.float32
    )
    fresh_up = train_up.astype(jnp.float32) + mix_rate * jnp.dot(
        low_up, high_up, preferred_element_type=jnp.float32
    )
    fresh_down = train_down.astype(jnp.float32) + mix_rate * jnp.dot(
        low_down, high_down, preferred_element_type=jnp.float32
    )
    narrow_gate, narrow_up, narrow_down = (
        fresh_gate.astype(jnp.bfloat16),
        fresh_up.astype(jnp.bfloat16),
        fresh_down.astype(jnp.bfloat16),
    )
    serve_gate, serve_up, serve_down = (
        lax.all_gather(narrow_gate, "zero", axis=0, tiled=True),
        lax.all_gather(narrow_up, "zero", axis=0, tiled=True),
        lax.all_gather(narrow_down, "zero", axis=1, tiled=True),
    )
    serve_gate, serve_up, serve_down = (serve_gate.T, serve_up.T, serve_down.T)
    serve_norm = lax.all_gather(
        (norm_train + norm_step).astype(jnp.bfloat16), ("zero", "tp"), axis=0, tiled=True
    )
    return (serve_gate, serve_up, serve_down, serve_norm)


def solution(mesh):
    return jax.shard_map(
        per_device,
        mesh=mesh,
        in_specs=(
            P("zero", "tp"),
            P("zero", None),
            P(None, "tp"),
            P("zero", "tp"),
            P("zero", None),
            P(None, "tp"),
            P("tp", "zero"),
            P("tp", None),
            P(None, "zero"),
            P(("zero", "tp")),
            P(("zero", "tp")),
        ),
        out_specs=(P("tp", None), P("tp", None), P(None, "tp"), P()),
        check_vma=False,
    )
```

profile of v0, /device:TPU:0, one launch (start us, length us, event | category | flops | bytes accessed | tf_op | source)
XLA Modules:
  0.0 567.8 jit_solution(18354530205563836709)
XLA Ops:
  7.2 0.0 copy-start
  7.2 0.0 copy-start.2
  7.2 0.0 copy-start.6
  7.2 0.0 copy-start.4
  7.2 0.0 all-gather.4.cloned.1.call-start
  7.3 0.8 copy-done
  8.0 3.2 add_convert_fusion.2
  11.2 0.0 copy-start.3
  11.2 0.0 all-gather.4.cloned.1.call-update
  11.2 0.0 all-gather.6.cloned.1.call-start
  11.3 0.0 copy-done.2
  11.3 0.0 copy-done.6
  11.3 0.0 copy-done.4
  11.3 1.7 add_convert_fusion.1
  13.0 0.0 all-gather.6.cloned.1.call-update
  13.0 0.0 all-gather.8.cloned.1.call-start
  13.1 0.0 copy-done.3
  13.1 0.0 copy-done.5
  13.1 0.0 copy-done.7
  13.1 1.8 add_convert_fusion
  14.9 0.0 all-gather.8.cloned.1.call-update
  14.9 0.0 copy-done.8
  14.9 0.0 copy-done.9
  15.0 0.2 dynamic-update-slice
  15.2 46.1 %all-reduce = bf16[3072]{0:T(1024)(128)(2,1)} all-reduce(bf16[3072]{0:T(1024)(128)(2,1)S(1)} %dynamic-update-slice), channel_id=1, replica_groups=mesh['zero'=8,'tp'=4] {'zero','tp'}, use_global_device_ids=true, to_apply=%add | all-reduce | flops 3072 | bytes 12288
  61.3 129.9 %all-gather.4.cloned.1.call-done = bf16[3072,2048]{1,0:T(8,128)(2,1)} async-done(((bf16[384,2048]{1,0:T(8,128)(2,1)}), bf16[3072,2048]{1,0:T(8,128)(2,1)}) %all-gather.4.cloned.1.call-update) | async-done | bytes 12582928 | tf_op jit(solution)/shard_map/all_gather | solution.py:37
  191.2 16.8 %copy.15 = bf16[2048,3072]{1,0:T(8,128)(2,1)} copy(bf16[2048,3072]{0,1:T(8,128)(2,1)} %bitcast.9) | data formatting | bytes 25165824
  207.9 160.3 %all-gather.6.cloned.1.call-done = bf16[3072,2048]{1,0:T(8,128)(2,1)} async-done(((bf16[384,2048]{1,0:T(8,128)(2,1)}), bf16[3072,2048]{1,0:T(8,128)(2,1)}) %all-gather.6.cloned.1.call-update) | async-done | bytes 12582928 | tf_op jit(solution)/shard_map/all_gather | solution.py:38
  368.3 16.8 %copy.16 = bf16[2048,3072]{1,0:T(8,128)(2,1)} copy(bf16[2048,3072]{0,1:T(8,128)(2,1)} %bitcast.10) | data formatting | bytes 25165824
  385.1 159.6 %all-gather.8.cloned.1.call-done = bf16[2048,3072]{1,0:T(8,128)(2,1)} async-done(((bf16[2048,384]{1,0:T(8,128)(2,1)}), bf16[2048,3072]{1,0:T(8,128)(2,1)}) %all-gather.8.cloned.1.call-update) | async-done | bytes 12582928 | tf_op jit(solution)/shard_map/all_gather | solution.py:39
  544.7 16.6 %copy.17 = bf16[3072,2048]{1,0:T(8,128)(2,1)} copy(bf16[3072,2048]{0,1:T(8,128)(2,1)} %bitcast.11) | data formatting | bytes 25165824
  561.3 0.0 copy-done.1
  (7 shorter events, 0.0 us)
Async XLA Ops:
  7.2 0.8 copy-start
  7.2 4.1 copy-start.2
  7.2 4.1 copy-start.6
  7.2 4.1 copy-start.4
  7.2 184.0 %all-gather.4.cloned.1.call-start = ((), (), s32[]{:S(2)}) async-start(), calls=%async_computation | async-start | bytes 14155776 | tf_op jit(solution)/shard_map/all_gather | solution.py:37
  11.2 1.9 copy-start.3
  11.2 1.9 copy-start.5
  11.2 1.9 copy-start.7
  11.2 357.1 %all-gather.6.cloned.1.call-start = ((), (), s32[]{:S(2)}) async-start(), calls=%async_computation.1 | async-start | bytes 14155776 | tf_op jit(solution)/shard_map/all_gather | solution.py:38
  13.0 1.9 copy-start.8
  13.0 1.9 copy-start.9
  13.0 531.6 %all-gather.8.cloned.1.call-start = ((), (), s32[]{:S(2)}) async-start(), calls=%async_computation.2 | async-start | bytes 14155776 | tf_op jit(solution)/shard_map/all_gather | solution.py:39
  544.7 16.6 %copy-start.1 = (bf16[16,2048]{1,0:T(8,128)(2,1)S(1)}, bf16[16,2048]{1,0:T(8,128)(2,1)}, u32[]{:S(2)}) copy-start(bf16[16,2048]{1,0:T(8,128)(2,1)} %param.13) | copy-start | bytes 196612
Sparse Core Ops, SparseCore 0:
  11.3 179.8 all-gather.3
  193.9 174.2 all-gather.5
  370.3 174.2 all-gather.7
where the time goes:
time: 569 us; the launch traced here: 568 us
  waiting for transfers between devices  450 us (79%)
  local copies, waits for them, and re-layouts  51.2 us (9%)
  blocking collectives  46.1 us (8%)
  between operations  13.9 us (2%)
  matrix products  6.64 us (1%)
    all_gather x1, waiting for transfers between devices, per_device(): lax.all_gather(narrow_up, 'zero', axis=0, tiled=True)  160 us
    all_gather x1, waiting for transfers between devices, per_device(): lax.all_gather(narrow_down, 'zero', axis=1, tiled=True)  160 us
    all_gather x1, waiting for transfers between devices, per_device(): lax.all_gather(narrow_gate, 'zero', axis=0, tiled=True)  130 us
    unnamed x25, local copies, waits for them, and re-layouts  51.2 us
    unnamed x1, blocking collectives  46.1 us
  transfers between devices with their start and end apart: 3, of which 3 were waited for; matrix products, arithmetic and copies ran while one was open for 7% of the time, Pallas kernels for 0%

commit v1 on v0

v1 whole, which is shorter than its diff:
```python
import functools

import jax
import jax.numpy as jnp
from jax import lax
from jax.experimental import pallas as pl
from jax.experimental.pallas import tpu as pltpu
from jax.sharding import PartitionSpec as P

mix_rate = 0.5
CUTS = 8
PIECES = 3 * CUTS
CROSS = PIECES // 6
STAY = PIECES - CROSS
LINE = PIECES + CROSS
DEPTH = 4
LAG = 4
MESH = pl.DeviceIdType.MESH


def fresh(train, low, high):
    return train.astype(jnp.float32) + mix_rate * jnp.dot(
        low, high, preferred_element_type=jnp.float32
    )


def piece_of(j):
    return jnp.where(
        j < CUTS,
        j,
        jnp.where(j < STAY, j + CROSS, jnp.where(j < PIECES, j - STAY + CUTS, j - PIECES + CUTS)),
    )


def gather_kernel(
    Z, n, m,
    tg, lg, hg, tu, lu, hu, td, ld, hd, nv,
    og, ou, od, nb,
    us, ur, ds, dr, ys, yr, ns, nr, wg, wu, wd, keep,
):
    i, tp = lax.axis_index("zero"), lax.axis_index("tp")
    z, y = i // 2, i % 2
    me = i * m + tp
    depth, width = tg.shape
    cut = width // CUTS

    barrier = pltpu.get_barrier_semaphore()

    def greet(k, _):
        other = lax.rem(me + k, n * m)
        pl.semaphore_signal(
            barrier, inc=1, device_id={"zero": other // m, "tp": lax.rem(other, m)}, device_id_type=MESH
        )
        return 0

    lax.fori_loop(1, n * m, greet, 0)

    def rows_of(source):
        return pl.ds(pl.multiple_of(source * depth, 128), depth)

    def region(which, source, r):
        part = pl.ds(pl.multiple_of(r * cut, cut), cut)
        if which == 2:
            return od.at[rows_of(source), part]
        return (og, ou)[which].at[part, rows_of(source)]

    def own(which, r):
        part = pl.ds(pl.multiple_of(r * cut, cut), cut)
        return wd.at[:, part] if which == 2 else (wg, wu)[which].at[part, :]

    def compute(which, r):
        part = pl.ds(pl.multiple_of(r * cut, cut), cut)
        if which == 2:
            value = fresh(td[part, :], ld[part, :], hd[...])
        else:
            train, low, high = ((tg, lg, hg), (tu, lu, hu))[which]
            value = fresh(train[:, part], low[...], high[:, part])
        own(which, r)[...] = value.T.astype(jnp.bfloat16)

    def compute_range(which, first, last):
        def step(r, _):
            compute(which, r)
            return 0

        lax.fori_loop(first, last, step, 0)

    def start(piece, source, dest, send, recv):
        r = lax.rem(piece, CUTS)

        def go(src, dst):
            pltpu.make_async_remote_copy(
                src, dst, send, recv, device_id={"zero": dest}, device_id_type=MESH
            ).start()

        for which in range(3):
            @pl.when((piece // CUTS == which) & (source == i))
            def _():
                go(own(which, r), region(which, source, r))

            @pl.when((piece // CUTS == which) & (source != i))
            def _():
                go(region(which, source, r), region(which, source, r))

    def waiter(send, recv):
        ref = region(0, 0, 0)
        return pltpu.make_async_remote_copy(
            ref, ref, send, recv, device_id={"zero": i}, device_id_type=MESH
        )

    n_up = jnp.where(z < Z - 1, LINE * (z + 1), 0)
    n_down = jnp.where(z > 0, LINE * (Z - z), 0)
    n_up_in = LINE * z
    n_down_in = LINE * (Z - 1 - z)
    n_side = PIECES + STAY * (Z - 1)
    low_side = jnp.minimum(z, Z - 1 - z)

    def start_line(q, sign, send, recv):
        k, j = q // LINE, lax.rem(q, LINE)
        row = jnp.where(j < PIECES, y, 1 - y)
        start(piece_of(j), (z - sign * k) * 2 + row, (z + sign) * 2 + y, send.at[lax.rem(q, DEPTH)], recv.at[q])

    def start_up(q):
        @pl.when(q < n_up)
        def _():
            start_line(q, 1, us, ur)

    def start_down(q):
        @pl.when(q < n_down)
        def _():
            start_line(q, -1, ds, dr)

    def start_side(q):
        @pl.when(q < n_side)
        def _():
            later = jnp.maximum(q - PIECES, 0)
            b, j = later // STAY, lax.rem(later, STAY)
            paired = b < 2 * low_side
            k = jnp.where(paired, b // 2 + 1, b - low_side + 1)
            back = jnp.where(paired, lax.rem(b, 2) == 0, z > Z - 1 - z)
            source = jnp.where(q < PIECES, z, jnp.where(back, z - k, z + k))
            piece = jnp.where(q < PIECES, q, piece_of(j))
            start(piece, source * 2 + y, z * 2 + 1 - y, ys.at[lax.rem(q, DEPTH)], yr.at[q])

    nb[me] = nv[...]
    compute_range(0, 0, DEPTH + 1)
    pl.semaphore_wait(barrier, n * m - 1)

    def first(q, _):
        start_up(q)
        start_down(q)
        start_side(q)
        return 0

    lax.fori_loop(0, DEPTH, first, 0)
    compute_range(0, DEPTH + 1, CUTS)
    compute_range(1, 0, CUTS)
    compute_range(2, 0, CUTS)
    kept = [
        pltpu.make_async_copy(src, dst, keep.at[which])
        for which, (src, dst) in enumerate((
            (wg, og.at[:, rows_of(i)]), (wu, ou.at[:, rows_of(i)]), (wd, od.at[rows_of(i), :]),
        ))
    ]
    for copy in kept:
        copy.start()

    def norm_copy(k):
        other = lax.rem(me + k, n * m)
        return pltpu.make_async_remote_copy(
            nb.at[me], nb.at[me], ns.at[k], nr.at[me],
            device_id={"zero": other // m, "tp": lax.rem(other, m)}, device_id_type=MESH,
        )

    def norm_send(k, _):
        norm_copy(k).start()
        return 0

    lax.fori_loop(1, n * m, norm_send, 0)

    def step(t, _):
        p = t - LAG
        at = jnp.maximum(p, 0)

        @pl.when((p >= 0) & (p < n_up_in))
        def _():
            waiter(us.at[0], ur.at[at]).wait_recv()

        @pl.when((p >= 0) & (p < n_down_in))
        def _():
            waiter(ds.at[0], dr.at[at]).wait_recv()

        @pl.when((p >= 0) & (p < n_side))
        def _():
            waiter(ys.at[0], yr.at[at]).wait_recv()

        slot = lax.rem(t, DEPTH)

        @pl.when(t < n_up)
        def _():
            waiter(us.at[slot], ur.at[0]).wait_send()

        start_up(t + DEPTH)

        @pl.when(t < n_down)
        def _():
            waiter(ds.at[slot], dr.at[0]).wait_send()

        start_down(t + DEPTH)

        @pl.when(t < n_side)
        def _():
            waiter(ys.at[slot], yr.at[0]).wait_send()

        start_side(t + DEPTH)
        return 0

    steps = max(LINE * (Z - 1), PIECES + STAY * (Z - 1)) + LAG
    lax.fori_loop(0, steps, step, 0)

    def norm_wait(k, _):
        other = lax.rem(me + k, n * m)
        norm_copy(k).wait_send()
        pltpu.make_async_remote_copy(
            nb.at[other], nb.at[other], ns.at[k], nr.at[other],
            device_id={"zero": i}, device_id_type=MESH,
        ).wait_recv()
        return 0

    lax.fori_loop(1, n * m, norm_wait, 0)
    for copy in kept:
        copy.wait()


def fast(
    n, m,
    train_gate, low_gate, high_gate,
    train_up, low_up, high_up,
    train_down, low_down, high_down,
    norm_train, norm_step,
):
    depth, width = train_gate.shape
    Z = n // 2
    gain = norm_train + norm_step
    share = gain.shape[0]
    lanes = -(-share // 128) * 128
    nv = jnp.broadcast_to(jnp.pad(gain, (0, lanes - share))[None], (8, lanes))
    n_line, n_side = LINE * (Z - 1), PIECES + STAY * (Z - 1)
    dma = pltpu.SemaphoreType.DMA
    outs = pl.pallas_call(
        functools.partial(gather_kernel, Z, n, m),
        out_shape=(
            jax.ShapeDtypeStruct((width, n * depth), jnp.bfloat16),
            jax.ShapeDtypeStruct((width, n * depth), jnp.bfloat16),
            jax.ShapeDtypeStruct((n * depth, width), jnp.bfloat16),
            jax.ShapeDtypeStruct((n * m, 8, lanes), jnp.float32),
        ),
        in_specs=[pl.BlockSpec(memory_space=pltpu.VMEM)] * 10,
        out_specs=(pl.BlockSpec(memory_space=pl.ANY),) * 3 + (pl.BlockSpec(memory_space=pltpu.VMEM),),
        scratch_shapes=[
            dma((DEPTH,)), dma((n_line,)),
            dma((DEPTH,)), dma((n_line,)),
            dma((DEPTH,)), dma((n_side,)),
            dma((n * m,)), dma((n * m,)),
            pltpu.VMEM((width, depth), jnp.bfloat16),
            pltpu.VMEM((width, depth), jnp.bfloat16),
            pltpu.VMEM((depth, width), jnp.bfloat16),
            dma((3,)),
        ],
        compiler_params=pltpu.CompilerParams(
            collective_id=0, has_side_effects=True
        ),
    )(
        train_gate, low_gate, high_gate,
        train_up, low_up, high_up,
        train_down, low_down, high_down,
        nv,
    )
    serve_gate, serve_up, serve_down, norms = outs
    serve_norm = norms[:, 0, :share].reshape(-1).astype(jnp.bfloat16)
    return serve_gate, serve_up, serve_down, serve_norm


def plain(
    train_gate, low_gate, high_gate,
    train_up, low_up, high_up,
    train_down, low_down, high_down,
    norm_train, norm_step,
):
    serve_gate = lax.all_gather(
        fresh(train_gate, low_gate, high_gate).astype(jnp.bfloat16), "zero", axis=0, tiled=True
    ).T
    serve_up = lax.all_gather(
        fresh(train_up, low_up, high_up).astype(jnp.bfloat16), "zero", axis=0, tiled=True
    ).T
    serve_down = lax.all_gather(
        fresh(train_down, low_down, high_down).astype(jnp.bfloat16), "zero", axis=1, tiled=True
    ).T
    serve_norm = lax.all_gather(
        (norm_train + norm_step).astype(jnp.bfloat16), ("zero", "tp"), axis=0, tiled=True
    )
    return serve_gate, serve_up, serve_down, serve_norm


def per_device(n, m, *args):
    depth, width = args[0].shape
    fits = (
        n % 2 == 0
        and 2 <= n // 2 <= 4
        and depth % 128 == 0
        and width % (CUTS * 128) == 0
        and args[6].shape == (width, depth)
        and 6 * n * depth * width <= 40 * 1024 * 1024
    )
    return fast(n, m, *args) if fits else plain(*args)


def solution(mesh):
    return jax.shard_map(
        functools.partial(per_device, mesh.shape["zero"], mesh.shape["tp"]),
        mesh=mesh,
        in_specs=(
            P("zero", "tp"),
            P("zero", None),
            P(None, "tp"),
            P("zero", "tp"),
            P("zero", None),
            P(None, "tp"),
            P("tp", "zero"),
            P("tp", None),
            P(None, "zero"),
            P(("zero", "tp")),
            P(("zero", "tp")),
        ),
        out_specs=(P("tp", None), P("tp", None), P(None, "tp"), P()),
        check_vma=False,
    )
```

time: 569 us -> 406 us (0.71)
  waiting for transfers between devices: 450 us -> 0 us
  Pallas kernels: 0 us -> 371 us
  blocking collectives: 46.1 us -> 0 us
  local copies, waits for them, and re-layouts: 51.2 us -> 32.9 us
  between operations: 13.9 us -> 0.65 us
  matrix products: 6.64 us -> 0 us
    all_gather x3 -> x0, waiting for transfers between devices: 450 us -> none  [the longest x1 160 us: per_device(): lax.all_gather(narrow_up, 'zero', axis=0, tiled=True)]
    pallas_call x0 -> x1, Pallas kernels: none -> 371 us  [fast(): pl.pallas_call(functools.partial(gather_kernel, Z, n, m), out_shape=(jax....]
    unnamed x1 -> x0, blocking collectives: 46.1 us -> none
    unnamed x25 -> x14, local copies, waits for them, and re-layouts: 51.2 us -> 30.7 us
    dot_general x3 -> x0, matrix products: 6.64 us -> none  [the longest x1 3.16 us: per_device(): jnp.dot(low_gate, high_gate, preferred_element_type=jnp.float32)]
  transfers between devices with their start and end apart: 3 -> 0, of which waited for: 3 -> 0; matrix products, arithmetic and copies ran while one was open for 7% -> 0% of each run, Pallas kernels for 0% -> 0%
where the time goes in v1:
time: 406 us; the launch traced here: 405 us
  Pallas kernels  371 us (91%)
  local copies, waits for them, and re-layouts  32.9 us (8%)
    pallas_call x1, Pallas kernels, fast(): pl.pallas_call(functools.partial(gather_kernel, Z, n, m), out_shape=(jax....  371 us
    unnamed x14, local copies, waits for them, and re-layouts  30.7 us

profile of v1, /device:TPU:0, one launch (start us, length us, event | category | flops | bytes accessed | tf_op | source)
XLA Modules:
  0.0 405.5 jit_solution(3802230568619239965)
XLA Ops:
  0.6 0.7 add.5
  1.3 0.6 broadcast_in_dim.2.nv
  1.9 1.4 copy.18.lg
  3.4 1.4 copy.19.lu
  4.8 1.8 copy.20.ld
  6.7 371.2 %shard_map.138 = (bf16[2048,3072]{1,0:T(8,128)(2,1)}, bf16[2048,3072]{1,0:T(8,128)(2,1)}, bf16[3072,2048]{1,0:T(8,128)(2,1)}, f32[32,8,128]{2,1,0:T(8,128)}) custom-call(bf16[384,2048]{1,0:T(8,128)(2,1)} %tg.1, bf16[384,16]{1,0:T(8,128)(2,1)} %copy.18.lg, bf16[16,2048]{1,0:T(8,128)(2,1)} %hg.1, bf16[384,2048]{1,0:T(8,128)(2,1)} %tu.1, ...), custom_call_target="tpu_custom_call" | custom-call | tf_op jit(solution)/shard_map/pallas_call | solution.py:249
  377.9 1.0 fusion
  378.8 0.7 convert_element_type.6
  379.5 0.0 copy-start
  379.5 0.0 slice-start
  379.5 0.0 slice-start.1
  379.5 12.4 %copy.24 = bf16[2048,3072]{1,0:T(8,128)(2,1)} copy(bf16[2048,3072]{1,0:T(8,128)(2,1)} %get-tuple-element.16) | data formatting | bytes 25165824
  391.9 0.0 copy-done
  391.9 0.0 slice-start.2
  392.0 6.4 %copy.25 = bf16[2048,3072]{1,0:T(8,128)(2,1)} copy(bf16[2048,3072]{1,0:T(8,128)(2,1)S(1)} %copy-done) | data formatting | bytes 25165824
  398.3 0.0 slice-done
  398.3 1.1 slice-done.1
  399.4 1.3 slice-done.2
  400.7 4.8 %copy.26 = bf16[3072,2048]{1,0:T(8,128)(2,1)} copy(bf16[3072,2048]{1,0:T(8,128)(2,1)S(1)} %bitcast.1) | data formatting | bytes 25165824
  (2 shorter events, 0.0 us)
Async XLA Ops:
  379.5 12.4 %copy-start = (bf16[2048,3072]{1,0:T(8,128)(2,1)S(1)}, bf16[2048,3072]{1,0:T(8,128)(2,1)}, u32[]{:S(2)}) copy-start(bf16[2048,3072]{1,0:T(8,128)(2,1)} %get-tuple-element.17) | copy-start | bytes 37748740
  379.5 18.8 %slice-start = ((s8[12582912]{0:T(1024)(128)(4,1)}), s8[4194304]{0:T(1024)(128)(4,1)S(1)}, s32[]{:S(2)}) async-start(s8[12582912]{0:T(1024)(128)(4,1)} %bitcast), calls=%async_computation | async-start | bytes 8388608
  379.5 19.9 %slice-start.1 = ((s8[12582912]{0:T(1024)(128)(4,1)}), s8[4194304]{0:T(1024)(128)(4,1)S(1)}, s32[]{:S(2)}) async-start(s8[12582912]{0:T(1024)(128)(4,1)} %bitcast), calls=%async_computation.1 | async-start | bytes 8388608
  391.9 8.8 %slice-start.2 = ((s8[12582912]{0:T(1024)(128)(4,1)}), s8[4194304]{0:T(1024)(128)(4,1)S(1)}, s32[]{:S(2)}) async-start(s8[12582912]{0:T(1024)(128)(4,1)} %bitcast), calls=%async_computation.2 | async-start | bytes 8388608

commit v2 on v1

--- a/solution.py
+++ b/solution.py
@@ -14,13 +14,14 @@
 STAY = PIECES - CROSS
 LINE = PIECES + CROSS
 DEPTH = 4
+AHEAD = 2
 LAG = 4
 MESH = pl.DeviceIdType.MESH
 
 
-def fresh(train, low, high):
-    return train.astype(jnp.float32) + mix_rate * jnp.dot(
-        low, high, preferred_element_type=jnp.float32
+def fresh(train, low_t, high):
+    return train.astype(jnp.float32) + mix_rate * lax.dot_general(
+        low_t, high, (((0,), (0,)), ((), ())), preferred_element_type=jnp.float32
     )
 
 
@@ -34,9 +35,9 @@
 
 def gather_kernel(
     Z, n, m,
-    tg, lg, hg, tu, lu, hu, td, ld, hd, nv,
-    og, ou, od, nb,
-    us, ur, ds, dr, ys, yr, ns, nr, wg, wu, wd, keep,
+    tg, lg, hg, tu, lu, hu, td, ld, hd, nt, nd,
+    held, nb,
+    us, ur, ds, dr, ys, yr, ns, nr, vu, vd, fetch,
 ):
     i, tp = lax.axis_index("zero"), lax.axis_index("tp")
     z, y = i // 2, i % 2
@@ -44,6 +45,10 @@
     depth, width = tg.shape
     cut = width // CUTS
 
+    fetch_up = pltpu.make_async_copy(tu, vu, fetch.at[0])
+    fetch_down = pltpu.make_async_copy(td, vd, fetch.at[1])
+    fetch_up.start()
+    fetch_down.start()
     barrier = pltpu.get_barrier_semaphore()
 
     def greet(k, _):
@@ -55,27 +60,27 @@
 
     lax.fori_loop(1, n * m, greet, 0)
 
-    def rows_of(source):
-        return pl.ds(pl.multiple_of(source * depth, 128), depth)
+    tiles = depth // 128
 
     def region(which, source, r):
-        part = pl.ds(pl.multiple_of(r * cut, cut), cut)
-        if which == 2:
-            return od.at[rows_of(source), part]
-        return (og, ou)[which].at[part, rows_of(source)]
-
-    def own(which, r):
-        part = pl.ds(pl.multiple_of(r * cut, cut), cut)
-        return wd.at[:, part] if which == 2 else (wg, wu)[which].at[part, :]
+        return held.at[which, pl.ds(source * tiles, tiles), pl.ds(pl.multiple_of(r * cut, cut), cut), :]
 
     def compute(which, r):
         part = pl.ds(pl.multiple_of(r * cut, cut), cut)
         if which == 2:
-            value = fresh(td[part, :], ld[part, :], hd[...])
+            value = fresh(vd[part, :], ld[:, part], hd[...])
         else:
-            train, low, high = ((tg, lg, hg), (tu, lu, hu))[which]
+            train, low, high = ((tg, lg, hg), (vu, lu, hu))[which]
             value = fresh(train[:, part], low[...], high[:, part])
-        own(which, r)[...] = value.T.astype(jnp.bfloat16)
+        served = value.T.astype(jnp.bfloat16)
+        for a in range(tiles):
+            if which == 2:
+                for b in range(cut // 128):
+                    held[2, i * tiles + a, pl.ds(pl.multiple_of(r * cut + b * 128, 128), 128), :] = (
+                        served[a * 128 : (a + 1) * 128, b * 128 : (b + 1) * 128]
+                    )
+            else:
+                held[which, i * tiles + a, part, :] = served[:, a * 128 : (a + 1) * 128]
 
     def compute_range(which, first, last):
         def step(r, _):
@@ -85,21 +90,10 @@
         lax.fori_loop(first, last, step, 0)
 
     def start(piece, source, dest, send, recv):
-        r = lax.rem(piece, CUTS)
-
-        def go(src, dst):
-            pltpu.make_async_remote_copy(
-                src, dst, send, recv, device_id={"zero": dest}, device_id_type=MESH
-            ).start()
-
-        for which in range(3):
-            @pl.when((piece // CUTS == which) & (source == i))
-            def _():
-                go(own(which, r), region(which, source, r))
-
-            @pl.when((piece // CUTS == which) & (source != i))
-            def _():
-                go(region(which, source, r), region(which, source, r))
+        ref = region(piece // CUTS, source, lax.rem(piece, CUTS))
+        pltpu.make_async_remote_copy(
+            ref, ref, send, recv, device_id={"zero": dest}, device_id_type=MESH
+        ).start()
 
     def waiter(send, recv):
         ref = region(0, 0, 0)
@@ -141,29 +135,24 @@
             piece = jnp.where(q < PIECES, q, piece_of(j))
             start(piece, source * 2 + y, z * 2 + 1 - y, ys.at[lax.rem(q, DEPTH)], yr.at[q])
 
-    nb[me] = nv[...]
-    compute_range(0, 0, DEPTH + 1)
+    nb[me] = jnp.zeros(nb.shape[1:], nb.dtype)
+    nb[me, 0:1, : nt.shape[1]] = nt[...] + nd[...]
+    compute_range(0, 0, AHEAD)
     pl.semaphore_wait(barrier, n * m - 1)
 
     def first(q, _):
         start_up(q)
         start_down(q)
         start_side(q)
+        compute(0, q + AHEAD)
         return 0
 
     lax.fori_loop(0, DEPTH, first, 0)
-    compute_range(0, DEPTH + 1, CUTS)
+    compute_range(0, DEPTH + AHEAD, CUTS)
+    fetch_up.wait()
     compute_range(1, 0, CUTS)
+    fetch_down.wait()
     compute_range(2, 0, CUTS)
-    kept = [
-        pltpu.make_async_copy(src, dst, keep.at[which])
-        for which, (src, dst) in enumerate((
-            (wg, og.at[:, rows_of(i)]), (wu, ou.at[:, rows_of(i)]), (wd, od.at[rows_of(i), :]),
-        ))
-    ]
-    for copy in kept:
-        copy.start()
-
     def norm_copy(k):
         other = lax.rem(me + k, n * m)
         return pltpu.make_async_remote_copy(
@@ -227,8 +216,23 @@
         return 0
 
     lax.fori_loop(1, n * m, norm_wait, 0)
-    for copy in kept:
-        copy.wait()
+
+
+def settle_kernel(held, og, ou, od, done):
+    _, groups, width, _ = held.shape
+
+    def group(c, _):
+        span = pl.ds(pl.multiple_of(c * 128, 128), 128)
+        pltpu.make_async_copy(held.at[0, c], og.at[:, span], done.at[0]).start()
+        pltpu.make_async_copy(held.at[1, c], ou.at[:, span], done.at[1]).start()
+        for d in range(width // 128):
+            part = pl.ds(d * 128, 128)
+            pltpu.make_async_copy(held.at[2, c, part, :], od.at[span, part], done.at[2]).start()
+        return 0
+
+    lax.fori_loop(0, groups, group, 0)
+    for k, ref in enumerate((og, ou, od)):
+        pltpu.make_async_copy(ref, ref, done.at[k]).wait()
 
 
 def fast(
@@ -240,42 +244,50 @@
 ):
     depth, width = train_gate.shape
     Z = n // 2
-    gain = norm_train + norm_step
-    share = gain.shape[0]
+    share = norm_train.shape[0]
     lanes = -(-share // 128) * 128
-    nv = jnp.broadcast_to(jnp.pad(gain, (0, lanes - share))[None], (8, lanes))
     n_line, n_side = LINE * (Z - 1), PIECES + STAY * (Z - 1)
     dma = pltpu.SemaphoreType.DMA
-    outs = pl.pallas_call(
+    held, norms = pl.pallas_call(
         functools.partial(gather_kernel, Z, n, m),
         out_shape=(
-            jax.ShapeDtypeStruct((width, n * depth), jnp.bfloat16),
-            jax.ShapeDtypeStruct((width, n * depth), jnp.bfloat16),
-            jax.ShapeDtypeStruct((n * depth, width), jnp.bfloat16),
+            pltpu.VMEM((3, n * depth // 128, width, 128), jnp.bfloat16),
             jax.ShapeDtypeStruct((n * m, 8, lanes), jnp.float32),
         ),
-        in_specs=[pl.BlockSpec(memory_space=pltpu.VMEM)] * 10,
-        out_specs=(pl.BlockSpec(memory_space=pl.ANY),) * 3 + (pl.BlockSpec(memory_space=pltpu.VMEM),),
+        in_specs=[
+            pl.BlockSpec(memory_space=pl.ANY if k in (3, 6) else pltpu.VMEM) for k in range(11)
+        ],
+        out_specs=(pl.BlockSpec(memory_space=pltpu.VMEM),) * 2,
         scratch_shapes=[
             dma((DEPTH,)), dma((n_line,)),
             dma((DEPTH,)), dma((n_line,)),
             dma((DEPTH,)), dma((n_side,)),
             dma((n * m,)), dma((n * m,)),
-            pltpu.VMEM((width, depth), jnp.bfloat16),
-            pltpu.VMEM((width, depth), jnp.bfloat16),
-            pltpu.VMEM((depth, width), jnp.bfloat16),
-            dma((3,)),
+            pltpu.VMEM(train_up.shape, jnp.bfloat16),
+            pltpu.VMEM(train_down.shape, jnp.bfloat16),
+            dma((2,)),
         ],
         compiler_params=pltpu.CompilerParams(
-            collective_id=0, has_side_effects=True
+            collective_id=0, has_side_effects=True, vmem_limit_bytes=27 * 1024 * 1024
         ),
     )(
-        train_gate, low_gate, high_gate,
-        train_up, low_up, high_up,
-        train_down, low_down, high_down,
-        nv,
-    )
-    serve_gate, serve_up, serve_down, norms = outs
+        train_gate, low_gate.T, high_gate,
+        train_up, low_up.T, high_up,
+        train_down, low_down.T, high_down,
+        norm_train[None], norm_step[None],
+    )
+    serve_gate, serve_up, serve_down = pl.pallas_call(
+        settle_kernel,
+        out_shape=(
+            jax.ShapeDtypeStruct((width, n * depth), jnp.bfloat16),
+            jax.ShapeDtypeStruct((width, n * depth), jnp.bfloat16),
+            jax.ShapeDtypeStruct((n * depth, width), jnp.bfloat16),
+        ),
+        in_specs=[pl.BlockSpec(memory_space=pltpu.VMEM)],
+        out_specs=(pl.BlockSpec(memory_space=pl.ANY),) * 3,
+        scratch_shapes=[dma((3,))],
+        compiler_params=pltpu.CompilerParams(vmem_limit_bytes=1024 * 1024),
+    )(pltpu.with_memory_space_constraint(held, pltpu.VMEM))
     serve_norm = norms[:, 0, :share].reshape(-1).astype(jnp.bfloat16)
     return serve_gate, serve_up, serve_down, serve_norm
 
@@ -287,13 +299,13 @@
     norm_train, norm_step,
 ):
     serve_gate = lax.all_gather(
-        fresh(train_gate, low_gate, high_gate).astype(jnp.bfloat16), "zero", axis=0, tiled=True
+        fresh(train_gate, low_gate.T, high_gate).astype(jnp.bfloat16), "zero", axis=0, tiled=True
     ).T
     serve_up = lax.all_gather(
-        fresh(train_up, low_up, high_up).astype(jnp.bfloat16), "zero", axis=0, tiled=True
+        fresh(train_up, low_up.T, high_up).astype(jnp.bfloat16), "zero", axis=0, tiled=True
     ).T
     serve_down = lax.all_gather(
-        fresh(train_down, low_down, high_down).astype(jnp.bfloat16), "zero", axis=1, tiled=True
+        fresh(train_down, low_down.T, high_down).astype(jnp.bfloat16), "zero", axis=1, tiled=True
     ).T
     serve_norm = lax.all_gather(
         (norm_train + norm_step).astype(jnp.bfloat16), ("zero", "tp"), axis=0, tiled=True

time: 406 us -> 384 us (0.946)
  local copies, waits for them, and re-layouts: 32.9 us -> 1.64 us
  Pallas kernels: 371 us -> 382 us
    unnamed x14 -> x0, local copies, waits for them, and re-layouts: 30.7 us -> none
    pallas_call x1 -> x2, Pallas kernels: 371 us -> 382 us  [the longest x1 370 us: fast(): pl.pallas_call(functools.partial(gather_kernel, Z, n, m), out_shape=(pltp...]
where the time goes in v2:
time: 384 us
  Pallas kernels  382 us (99%)
    pallas_call x1, Pallas kernels, fast(): pl.pallas_call(functools.partial(gather_kernel, Z, n, m), out_shape=(pltp...  370 us
    pallas_call x1, Pallas kernels, fast(): pl.pallas_call(settle_kernel, out_shape=(jax.ShapeDtypeStruct((width, n *...  11.9 us

profile of v2, /device:TPU:0, one launch (start us, length us, event | category | flops | bytes accessed | tf_op | source)
XLA Modules:
  0.0 384.3 jit_solution(7076649515102195586)
XLA Ops:
  0.6 370.0 %shard_map.138 = (bf16[3,24,2048,128]{3,2,1,0:T(8,128)(2,1)S(1)}, f32[32,8,128]{2,1,0:T(8,128)}) custom-call(bf16[384,2048]{1,0:T(8,128)(2,1)} %tg.1, bf16[16,384]{1,0:T(8,128)(2,1)} %bitcast.6, bf16[16,2048]{1,0:T(8,128)(2,1)} %hg.1, bf16[384,2048]{1,0:T(8,128)(2,1)} %tu.1, bf16[16,384]{1,0:T(8,128)(2,1)} %bitcast.7, bf16[16,2048]{1,0:T(8,128)(2,1)} %hu.1, ...), custom_call_target="tpu_custom_call" | custom-call | tf_op jit(solution)/shard_map/pallas_call | solution.py:251
  370.7 11.9 %shard_map.139 = (bf16[2048,3072]{1,0:T(8,128)(2,1)}, bf16[2048,3072]{1,0:T(8,128)(2,1)}, bf16[3072,2048]{1,0:T(8,128)(2,1)}) custom-call(bf16[3,24,2048,128]{3,2,1,0:T(8,128)(2,1)S(1)} %get-tuple-element.9.held), custom_call_target="tpu_custom_call" | custom-call | tf_op jit(solution)/shard_map/pallas_call | solution.py:279
  382.6 1.0 fusion
  383.6 0.7 convert_element_type.4

commit v3 on v2

--- a/solution.py
+++ b/solution.py
@@ -8,14 +8,14 @@
 from jax.sharding import PartitionSpec as P
 
 mix_rate = 0.5
-CUTS = 8
+CUTS = 16
 PIECES = 3 * CUTS
 CROSS = PIECES // 6
 STAY = PIECES - CROSS
 LINE = PIECES + CROSS
-DEPTH = 4
+DEPTH = 6
 AHEAD = 2
-LAG = 4
+LAG = 6
 MESH = pl.DeviceIdType.MESH
 
 

time: 384 us -> 389 us (1.013)
  Pallas kernels: 382 us -> 386 us
    pallas_call x1, Pallas kernels: 370 us -> 375 us  [fast(): pl.pallas_call(functools.partial(gather_kernel, Z, n, m), out_shape=(pltp...]
where the time goes in v3:
time: 389 us
  Pallas kernels  386 us (99%)
    pallas_call x1, Pallas kernels, fast(): pl.pallas_call(functools.partial(gather_kernel, Z, n, m), out_shape=(pltp...  375 us
    pallas_call x1, Pallas kernels, fast(): pl.pallas_call(settle_kernel, out_shape=(jax.ShapeDtypeStruct((width, n *...  11.9 us

profile of v3, /device:TPU:0, one launch (start us, length us, event | category | flops | bytes accessed | tf_op | source)
XLA Modules:
  0.0 388.8 jit_solution(11810829302628213340)
XLA Ops:
  0.6 374.5 %shard_map.138 = (bf16[3,24,2048,128]{3,2,1,0:T(8,128)(2,1)S(1)}, f32[32,8,128]{2,1,0:T(8,128)}) custom-call(bf16[384,2048]{1,0:T(8,128)(2,1)} %tg.1, bf16[16,384]{1,0:T(8,128)(2,1)} %bitcast.6, bf16[16,2048]{1,0:T(8,128)(2,1)} %hg.1, bf16[384,2048]{1,0:T(8,128)(2,1)} %tu.1, bf16[16,384]{1,0:T(8,128)(2,1)} %bitcast.7, bf16[16,2048]{1,0:T(8,128)(2,1)} %hu.1, ...), custom_call_target="tpu_custom_call" | custom-call | tf_op jit(solution)/shard_map/pallas_call | solution.py:251
  375.2 11.9 %shard_map.139 = (bf16[2048,3072]{1,0:T(8,128)(2,1)}, bf16[2048,3072]{1,0:T(8,128)(2,1)}, bf16[3072,2048]{1,0:T(8,128)(2,1)}) custom-call(bf16[3,24,2048,128]{3,2,1,0:T(8,128)(2,1)S(1)} %get-tuple-element.9.held), custom_call_target="tpu_custom_call" | custom-call | tf_op jit(solution)/shard_map/pallas_call | solution.py:279
  387.1 1.0 fusion
  388.1 0.7 convert_element_type.4
